TPU v7x, 32 devices: a whole 2x2x4 slice. The times are simulated.
32 devices in a mesh: dp: 4 (over z), vocab: 8 (over y, x, core).
Axes of the slice: x: 2, y: 2, z: 4, core: 2. Of those that a mesh axis runs over, the one named last changes fastest.
Arguments:
- hidden: bfloat16 [512, 4096], P(('dp', 'vocab')), may hold values from -64 to 64
- head_weight: bfloat16 [4096, 128256], P(None, ('dp', 'vocab')), may hold values from -0.0625 to 0.0625
- targets: int32 [512], P(('dp', 'vocab')), may hold values from 0 to 128255
- bench_ids: int32 [512], P(('dp', 'vocab')), may hold values from 0 to 39, as said below
- valid: int32 [512], P(('dp', 'vocab')), may hold values from 0 to 1, as said below
- seq_lengths: int32 [16], replicated, may hold values from 1 to 64, 512 in all
Outputs:
- token_loss: float32 [512], P(('dp', 'vocab'))
- bench_loss: float32 [40], replicated
- bench_count: float32 [40], replicated
Inputs may be any that keep to these rules, and one draw needn't show every extreme that they name: `valid`: among the 16 positions of one device (aligned blocks) at most 8 have validity 1, and some block has exactly 8. `bench_ids`: A benchmark may have no positions in the window.
All inputs are finite; a program needn't handle non-finite values.
Results may differ from a plain program's by a relative error of at most 0.0003.
Values may be sent and summed in bfloat16 or wider, within the bound.
A program may use at most 128 MiB of HBM per device.

v0:
```python
import jax
import jax.numpy as jnp
from jax import lax
from jax.sharding import PartitionSpec as P

BENCH = 40


def body(hidden, head_weight, targets, bench_ids, valid, seq_lengths):
    row_count = hidden.shape[0]
    col_width = head_weight.shape[1]
    device_index = lax.axis_index(("dp", "vocab"))
    col_offset = device_index * col_width
    seq_ends = jnp.cumsum(seq_lengths) - 1
    positions = device_index * row_count + jnp.arange(row_count, dtype=jnp.int32)
    is_end = jnp.any(positions[:, None] == seq_ends[None, :], axis=1)
    scored = valid * (1 - is_end.astype(jnp.int32))
    scored_float = scored.astype(jnp.float32)
    labels = jnp.stack([targets, bench_ids, scored], axis=1)
    gathered_rows = row_count * lax.axis_size(("dp", "vocab"))
    column_ids = jnp.arange(col_width, dtype=jnp.int32)
    empty = jnp.zeros((gathered_rows,), jnp.float32)
    empty_labels = jnp.zeros((gathered_rows, 3), jnp.int32)
    block_rows = lax.all_gather(hidden, ("dp", "vocab"), axis=0, tiled=True)
    block_labels = lax.all_gather(labels, ("dp", "vocab"), axis=0, tiled=True)
    logits = jnp.dot(block_rows, head_weight, preferred_element_type=jnp.float32)
    row_top = jnp.max(logits, axis=1)
    row_total = jnp.sum(jnp.exp(logits - row_top[:, None]), axis=1)
    local_ids = block_labels[:, 0] - col_offset
    hits = column_ids[None, :] == local_ids[:, None]
    target_logit = jnp.sum(jnp.where(hits, logits, 0.0), axis=1)
    row_top, row_total, target_logit, all_labels = (
        row_top,
        row_total,
        target_logit,
        lax.dynamic_update_slice_in_dim(
            (empty, empty, empty, empty_labels)[3], block_labels, jnp.int32(0), 0
        ),
    )
    best = lax.pmax(row_top, ("dp", "vocab"))
    summed, target_sum = lax.psum(
        (row_total * jnp.exp(row_top - best), target_logit), ("dp", "vocab")
    )
    all_losses = best + jnp.log(summed) - target_sum
    own_losses = lax.dynamic_slice_in_dim(all_losses, device_index * row_count, row_count)
    token_loss = own_losses * scored_float
    bench_range = jnp.arange(BENCH, dtype=jnp.int32)
    scored_all = all_labels[:, 2].astype(jnp.float32)
    onehot_all = (all_labels[:, 1][:, None] == bench_range[None, :]).astype(jnp.float32)
    loss_sums = jnp.sum(onehot_all * (all_losses * scored_all)[:, None], axis=0)
    token_counts = jnp.sum(onehot_all * scored_all[:, None], axis=0)
    bench_loss = loss_sums / jnp.maximum(token_counts, 1.0)
    return (token_loss, bench_loss, token_counts)


def solution(mesh):
    placed = (
        P(("dp", "vocab"), None),
        P(None, ("dp", "vocab")),
        P(("dp", "vocab")),
        P(("dp", "vocab")),
        P(("dp", "vocab")),
        P(),
    )
    return jax.shard_map(
        body, mesh=mesh, in_specs=placed, out_specs=(P(("dp", "vocab")), P(), P()), check_vma=False
    )
```

profile of v0, /device:TPU:0, one launch (start us, length us, event | category | flops | bytes accessed | tf_op | source)
XLA Modules:
  0.0 190.8 jit_solution(16473174855132264849)
XLA Ops:
  7.2 0.0 all-gather.3.cloned.1.call-start
  7.2 0.7 all-gather.3.cloned.1.call-update
  7.9 0.7 copy.14
  8.7 0.1 add_reduce_fusion
  8.8 0.2 compare_reduce_fusion
  9.0 0.7 fusion
  9.6 0.7 add_bitcast_fusion
  10.3 43.7 %all-gather = s32[32,16,3]{1,2,0:T(4,128)S(1)} all-gather(s32[1,16,3]{1,2,0:T(4,128)S(1)} %add_bitcast_fusion), channel_id=1, replica_groups=mesh['dp'=4,'vocab'=8] {'dp','vocab'}, dimensions={0}, use_global_device_ids=true | all-gather | bytes 6336 | tf_op jit(solution)/shard_map/all_gather | solution.py:25
  54.0 0.1 reshape.42
  54.1 21.3 %all-gather.3.cloned.1.call-done = bf16[512,4096]{1,0:T(8,128)(2,1)} async-done(((bf16[16,4096]{1,0:T(8,128)(2,1)}), bf16[512,4096]{1,0:T(8,128)(2,1)}) %all-gather.3.cloned.1.call-update) | async-done | bytes 4194320 | tf_op jit(solution)/shard_map/all_gather | solution.py:24
  75.4 23.7 %fusion.3 = (f32[512]{0:T(512)S(1)}, f32[512,4008]{0,1:T(8,128)}) fusion(bf16[512,4096]{1,0:T(8,128)(2,1)} %all-gather.3.cloned.1.call-done, bf16[4096,4008]{0,1:T(8,128)(2,1)} %param.7), kind=kOutput, calls=%fused_computation.20 | convolution fusion | flops 16812822528 | bytes 45238272 | tf_op jit(solution)/shard_map/dot_general | solution.py:26
  99.1 0.0 copy-start.1
  99.1 39.1 %pmax.7 = f32[512]{0:T(512)S(1)} all-reduce(f32[512]{0:T(512)S(1)} %get-tuple-element.14), channel_id=1, replica_groups=mesh['dp'=4,'vocab'=8] {'dp','vocab'}, use_global_device_ids=true, to_apply=%region_1.2 | all-reduce | flops 512 | bytes 4096 | tf_op jit(solution)/shard_map/pmax | solution.py:40
  138.2 4.5 %exponential_reduce_fusion = (f32[512]{0:T(512)S(1)}, f32[512]{0:T(512)S(1)}) fusion(f32[512,4008]{0,1:T(8,128)} %get-tuple-element.15, f32[512]{0:T(512)S(1)} %get-tuple-element.14, s32[512]{0:T(512)S(1)} %bitcast.16), kind=kLoop, calls=%fused_computation.2 | loop fusion | flops 10259456 | bytes 8216576 | tf_op jit(solution)/shard_map/reduce_sum | solution.py:28
  142.7 40.0 %all-reduce = (f32[512]{0:T(512)S(1)}, f32[512]{0:T(512)S(1)}) all-reduce(f32[512]{0:T(512)S(1)} %get-tuple-element.4, f32[512]{0:T(512)S(1)} %exponential_multiply_fusion), channel_id=1, replica_groups=mesh['dp'=4,'vocab'=8] {'dp','vocab'}, use_global_device_ids=true, to_apply=%region_7.8 | all-reduce | flops 1024 | bytes 8192 | tf_op jit(solution)/shard_map/psum | solution.py:41
  182.7 0.0 copy-done.1
  182.7 0.6 convert_multiply_fusion
  183.3 0.1 select_reduce_fusion.1
  183.4 0.0 copy-start
  183.4 0.5 maximum_divide_fusion
  183.9 0.0 copy-done
  (6 shorter events, 0.1 us)
Async XLA Ops:
  7.2 68.2 %all-gather.3.cloned.1.call-start = ((), (), s32[]{:S(2)}) async-start(), calls=%async_computation | async-start | bytes 4325376 | tf_op jit(solution)/shard_map/all_gather | solution.py:24
  99.1 83.6 %copy-start.1 = (s32[16]{0:T(128)S(1)}, s32[16]{0:T(128)}, u32[]{:S(2)}) copy-start(s32[16]{0:T(128)} %param.10) | copy-start | bytes 196
  183.4 0.5 copy-start
Sparse Core Ops, SparseCore 0:
  10.8 64.4 all-gather.2
where the time goes:
time: 191 us
  blocking collectives  123 us (64%)
  matrix products  23.7 us (12%)
  waiting for transfers between devices  21.9 us (11%)
  between operations  14.1 us (7%)
  other arithmetic  7.44 us (4%)
    all_gather x1, blocking collectives, body(): block_labels = lax.all_gather(labels, ('dp', 'vocab'), axis=0, tiled=True)  43.7 us
    psum x1, blocking collectives, body(): lax.psum((row_total * jnp.exp(row_top - best), target_logit), ('dp', 'voc...  40 us
    pmax x1, blocking collectives, body(): best = lax.pmax(row_top, ('dp', 'vocab'))  39.1 us
    dot_general x1, matrix products, body(): jnp.dot(block_rows, head_weight, preferred_element_type=jnp.float32)  23.7 us
    all_gather x1, waiting for transfers between devices, body(): block_rows = lax.all_gather(hidden, ('dp', 'vocab'), axis=0, tiled=True)  21.3 us
    reduce_sum x1, other arithmetic, body(): row_total = jnp.sum(jnp.exp(logits - row_top[:, None]), axis=1)  4.49 us
  transfers between devices with their start and end apart: 1, of which 1 were waited for; matrix products, arithmetic and copies ran while one was open for 1% of the time, Pallas kernels for 0%

commit v1 on v0

--- a/solution.py
+++ b/solution.py
@@ -39,7 +39,7 @@
     )
     best = lax.pmax(row_top, ("dp", "vocab"))
     summed, target_sum = lax.psum(
-        (row_total * jnp.exp(row_top - best), target_logit), ("dp", "vocab")
+        lax.psum((row_total * jnp.exp(row_top - best), target_logit), "vocab"), "dp"
     )
     all_losses = best + jnp.log(summed) - target_sum
     own_losses = lax.dynamic_slice_in_dim(all_losses, device_index * row_count, row_count)

time: 191 us -> 174 us (0.911)
  blocking collectives: 123 us -> 105 us
    psum x1 -> x2, blocking collectives: 40 us -> 22.7 us  [the longest x1 12.7 us: body(): lax.psum((row_total * jnp.exp(row_top - best), target_logit), 'vocab')]
where the time goes in v1:
time: 174 us; the launch traced here: 173 us
  blocking collectives  105 us (60%)
  matrix products  23.7 us (14%)
  waiting for transfers between devices  21.9 us (13%)
  between operations  14.1 us (8%)
  other arithmetic  7.44 us (4%)
    all_gather x1, blocking collectives, body(): block_labels = lax.all_gather(labels, ('dp', 'vocab'), axis=0, tiled=True)  43.7 us
    pmax x1, blocking collectives, body(): best = lax.pmax(row_top, ('dp', 'vocab'))  39.1 us
    dot_general x1, matrix products, body(): jnp.dot(block_rows, head_weight, preferred_element_type=jnp.float32)  23.7 us
    all_gather x1, waiting for transfers between devices, body(): block_rows = lax.all_gather(hidden, ('dp', 'vocab'), axis=0, tiled=True)  21.3 us
    psum x1, blocking collectives, body(): lax.psum((row_total * jnp.exp(row_top - best), target_logit), 'vocab')  12.7 us
    psum x1, blocking collectives, body(): lax.psum(lax.psum((row_total * jnp.exp(row_top - best), target_logit), 'v...  9.98 us
    reduce_sum x1, other arithmetic, body(): row_total = jnp.sum(jnp.exp(logits - row_top[:, None]), axis=1)  4.49 us
  transfers between devices with their start and end apart: 1, of which 1 were waited for; matrix products, arithmetic and copies ran while one was open for 1% of the time, Pallas kernels for 0%

profile of v1, /device:TPU:0, one launch (start us, length us, event | category | flops | bytes accessed | tf_op | source)
XLA Modules:
  0.0 173.5 jit_solution(8318934328188095848)
XLA Ops:
  7.2 0.0 all-gather.3.cloned.1.call-start
  7.2 0.7 all-gather.3.cloned.1.call-update
  7.9 0.7 copy.14
  8.7 0.1 add_reduce_fusion
  8.8 0.2 compare_reduce_fusion
  9.0 0.7 fusion
  9.6 0.7 add_bitcast_fusion
  10.3 43.7 %all-gather = s32[32,16,3]{1,2,0:T(4,128)S(1)} all-gather(s32[1,16,3]{1,2,0:T(4,128)S(1)} %add_bitcast_fusion), channel_id=1, replica_groups=mesh['dp'=4,'vocab'=8] {'dp','vocab'}, dimensions={0}, use_global_device_ids=true | all-gather | bytes 6336 | tf_op jit(solution)/shard_map/all_gather | solution.py:25
  54.0 0.1 reshape.42
  54.1 21.3 %all-gather.3.cloned.1.call-done = bf16[512,4096]{1,0:T(8,128)(2,1)} async-done(((bf16[16,4096]{1,0:T(8,128)(2,1)}), bf16[512,4096]{1,0:T(8,128)(2,1)}) %all-gather.3.cloned.1.call-update) | async-done | bytes 4194320 | tf_op jit(solution)/shard_map/all_gather | solution.py:24
  75.4 23.7 %fusion.3 = (f32[512]{0:T(512)S(1)}, f32[512,4008]{0,1:T(8,128)}) fusion(bf16[512,4096]{1,0:T(8,128)(2,1)} %all-gather.3.cloned.1.call-done, bf16[4096,4008]{0,1:T(8,128)(2,1)} %param.7), kind=kOutput, calls=%fused_computation.20 | convolution fusion | flops 16812822528 | bytes 45238272 | tf_op jit(solution)/shard_map/dot_general | solution.py:26
  99.1 0.0 copy-start.1
  99.1 39.1 %pmax.7 = f32[512]{0:T(512)S(1)} all-reduce(f32[512]{0:T(512)S(1)} %get-tuple-element.16), channel_id=1, replica_groups=mesh['dp'=4,'vocab'=8] {'dp','vocab'}, use_global_device_ids=true, to_apply=%region_1.2 | all-reduce | flops 512 | bytes 4096 | tf_op jit(solution)/shard_map/pmax | solution.py:40
  138.2 4.5 %exponential_reduce_fusion = (f32[512]{0:T(512)S(1)}, f32[512]{0:T(512)S(1)}) fusion(f32[512,4008]{0,1:T(8,128)} %get-tuple-element.17, f32[512]{0:T(512)S(1)} %get-tuple-element.16, s32[512]{0:T(512)S(1)} %bitcast.16), kind=kLoop, calls=%fused_computation.2 | loop fusion | flops 10259456 | bytes 8216576 | tf_op jit(solution)/shard_map/reduce_sum | solution.py:28
  142.7 12.7 %all-reduce = (f32[512]{0:T(512)S(1)}, f32[512]{0:T(512)S(1)}) all-reduce(f32[512]{0:T(512)S(1)} %get-tuple-element.4, f32[512]{0:T(512)S(1)} %exponential_multiply_fusion), channel_id=1, replica_groups=mesh['dp'=4,'vocab'=8] {'vocab'}, use_global_device_ids=true, to_apply=%region_8.9 | all-reduce | flops 1024 | bytes 8192 | tf_op jit(solution)/shard_map/psum | solution.py:42
  155.4 10.0 %all-reduce.1 = (f32[512]{0:T(512)S(1)}, f32[512]{0:T(512)S(1)}) all-reduce(f32[512]{0:T(512)S(1)} %get-tuple-element.7, f32[512]{0:T(512)S(1)} %get-tuple-element.8), channel_id=1, replica_groups=mesh['dp'=4,'vocab'=8] {'dp'}, use_global_device_ids=true, to_apply=%region_9.10 | all-reduce | flops 1024 | bytes 8192 | tf_op jit(solution)/shard_map/psum | solution.py:41
  165.4 0.0 copy-done.1
  165.4 0.6 convert_multiply_fusion
  166.0 0.1 select_reduce_fusion.1
  166.1 0.0 copy-start
  166.1 0.5 maximum_divide_fusion
  166.6 0.0 copy-done
  (6 shorter events, 0.1 us)
Async XLA Ops:
  7.2 68.2 %all-gather.3.cloned.1.call-start = ((), (), s32[]{:S(2)}) async-start(), calls=%async_computation | async-start | bytes 4325376 | tf_op jit(solution)/shard_map/all_gather | solution.py:24
  99.1 66.3 %copy-start.1 = (s32[16]{0:T(128)S(1)}, s32[16]{0:T(128)}, u32[]{:S(2)}) copy-start(s32[16]{0:T(128)} %param.10) | copy-start | bytes 196
  166.1 0.5 copy-start
Sparse Core Ops, SparseCore 0:
  10.8 64.4 all-gather.2
